TPU v7x, 32 devices: a whole 2x2x4 slice. The times are simulated.
32 devices in a mesh: head: 2 (over x), inner: 4 (over y, core), outer: 4 (over z).
Axes of the slice: x: 2, y: 2, z: 4, core: 2. Of those that a mesh axis runs over, the one named last changes fastest.
Arguments:
- queries: float32 [2048, 8, 128], P(('inner', 'outer'), 'head'), may hold values from -8 to 8
- key_rows: float32 [2048, 128], P(('inner', 'outer'), 'head'), may hold values from -8 to 8
- values: float32 [2048, 128], P(('inner', 'outer'), 'head'), may hold values from -24 to 24
- out_grad: float32 [2048, 8, 128], P(('inner', 'outer'), 'head'), may hold values from -48 to 48
- sink_len: int32 [1], replicated, may hold values from 32 to 128
- window_len: int32 [1], replicated, may hold values from 129 to 640
- block_codes: int32 [16, 5], replicated, may hold values from 0 to 2, as said below
Outputs:
- query_grad: float32 [2048, 8, 128], P(('inner', 'outer'), 'head')
- key_grad: float32 [2048, 128], P(('inner', 'outer'), 'head')
- value_grad: float32 [2048, 128], P(('inner', 'outer'), 'head')
Inputs may be any that keep to these rules, and one draw needn't show every extreme that they name: block_codes[b, 0] is 1 or 2 for every block b.
All inputs are finite; a program needn't handle non-finite values.
Results may differ from a plain program's by a relative error of at most 0.0003.
Values sent between devices are 32-bit elements; how exact they have to be, the bound alone decides.
A program may use at most 64 MiB of HBM per device.

v0:
```python
import math

import jax
import jax.numpy as jnp
from jax import lax
from jax.sharding import PartitionSpec as P

STEPS = 5
SINK = 128


very_low = -1e30
precise = lax.Precision.HIGHEST


def swapped(array, axis, distance):
    return lax.ppermute(array, axis, [(i, i ^ 1 << distance) for i in range(lax.axis_size(axis))])


def spread(array, axis, root):
    mine = lax.axis_index(axis) == root
    return lax.psum(jnp.where(mine, array, jnp.zeros_like(array)), axis)


def shifted(value, axis, steps):
    count = lax.axis_size(axis)
    pairs = [(source, (source + steps) % count) for source in range(count)]
    return lax.ppermute(value, axis, pairs)


def codes_for(block_codes, query_block, offset):
    row_ids = jnp.arange(block_codes.shape[0], dtype=jnp.int32)
    return jnp.sum(jnp.where(row_ids == query_block, block_codes[:, offset], 0))


def visible(query_block, key_block, offset, block_rows, sink_end, window, block_codes, present):
    local_ids = jnp.arange(block_rows, dtype=jnp.int32)
    pos_q = query_block * block_rows + local_ids
    pos_k = key_block * block_rows + local_ids
    code = codes_for(block_codes, query_block, offset)
    near = pos_q[:, None] - pos_k[None, :] < window
    rule = (code != 0) & ((code == 2) | near)
    in_sink = (pos_k < sink_end)[None, :]
    chosen = jnp.where(query_block == 0, in_sink | rule, jnp.logical_not(in_sink) & rule)
    return present & (pos_k[None, :] <= pos_q[:, None]) & chosen


def scores(query_blk, key_blk, temper):
    return temper * jnp.einsum("qhd,kd->hqk", query_blk, key_blk, precision=precise)


def forward_step(running, query_blk, key_blk, value_blk, allowed, temper):
    row_max, row_sum, carried = running
    logits = jnp.where(allowed[None], scores(query_blk, key_blk, temper), very_low)
    new_max = jnp.maximum(row_max, jnp.max(logits, axis=2))
    factor = jnp.exp(row_max - new_max)
    weights = jnp.where(allowed[None], jnp.exp(logits - new_max[:, :, None]), 0.0)
    row_sum = row_sum * factor + jnp.sum(weights, axis=2)
    carried = carried * factor[:, :, None] + jnp.einsum(
        "hqk,kd->hqd", weights, value_blk, precision=precise
    )
    return ((new_max, row_sum, carried), logits)


def finish(running, grad_blk):
    row_max, row_sum, carried = running
    log_sum = row_max + jnp.log(row_sum)
    row_delta = jnp.sum(jnp.transpose(grad_blk, (1, 0, 2)) * carried, axis=2) / row_sum
    return (log_sum, row_delta)


def backward_step(
    query_blk, grad_blk, log_sum, row_delta, key_blk, value_blk, allowed, temper, cached
):
    if cached is None:
        cached = scores(query_blk, key_blk, temper)
    weights = jnp.where(allowed[None], jnp.exp(cached - log_sum[:, :, None]), 0.0)
    grad_dots = jnp.einsum("qhd,kd->hqk", grad_blk, value_blk, precision=precise)
    dscores = weights * (grad_dots - row_delta[:, :, None])
    step_dq = temper * jnp.einsum("hqk,kd->qhd", dscores, key_blk, precision=precise)
    step_dk = temper * jnp.einsum("hqk,qhd->kd", dscores, query_blk, precision=precise)
    step_dv = jnp.einsum("hqk,qhd->kd", weights, grad_blk, precision=precise)
    return (step_dq, step_dk, step_dv)


def shards(queries, key_rows, values, out_grad, sink_len, window_len, block_codes):
    block_rows, heads_dev, head_dim = queries.shape
    temper = 1.0 / math.sqrt(head_dim)
    sink_end = sink_len[0]
    window = window_len[0]
    seq_index = lax.axis_index(("inner", "outer"))
    seq_count = lax.axis_size(("inner", "outer"))
    upper_half = lax.axis_index("head") % 2 == 1
    other_keys, other_values = swapped((key_rows, values), "head", 0)
    key_full = jnp.where(
        upper_half,
        jnp.concatenate([other_keys, key_rows], 1),
        jnp.concatenate([key_rows, other_keys], 1),
    )
    value_full = jnp.where(
        upper_half,
        jnp.concatenate([other_values, values], 1),
        jnp.concatenate([values, other_values], 1),
    )
    sink_keys, sink_values = (
        spread(key_full, ("inner", "outer"), 0),
        spread(value_full, ("inner", "outer"), 0),
    )
    sink_ids = jnp.arange(SINK, dtype=jnp.int32)
    sink_allowed = jnp.broadcast_to(
        ((seq_index >= 1) & (sink_ids < sink_end))[None, :], (block_rows, SINK)
    )
    carried = jnp.zeros((heads_dev, block_rows, head_dim), jnp.float32)
    running = (
        jnp.full((heads_dev, block_rows), very_low, jnp.float32),
        jnp.zeros((heads_dev, block_rows), jnp.float32),
        carried,
    )
    running, ignored = forward_step(running, queries, sink_keys, sink_values, sink_allowed, temper)
    grad_keys = jnp.zeros((block_rows, head_dim), jnp.float32)
    grad_values = jnp.zeros((block_rows, head_dim), jnp.float32)
    moving_k, moving_v = (key_full, value_full)
    cached = None
    for offset in range(STEPS):
        if offset > 0:
            moving_k, moving_v = shifted((moving_k, moving_v), ("inner", "outer"), 1)
        allowed = visible(
            seq_index,
            (seq_index - offset) % seq_count,
            offset,
            block_rows,
            sink_end,
            window,
            block_codes,
            seq_index - offset >= 0,
        )
        running, cached = forward_step(running, queries, moving_k, moving_v, allowed, temper)
    log_sum, row_delta = finish(running, out_grad)
    grad_q = jnp.zeros_like(queries)
    for offset in range(STEPS - 1, -1, -1):
        if offset < STEPS - 1:
            moving_k, moving_v, grad_keys, grad_values = shifted(
                (moving_k, moving_v, grad_keys, grad_values), ("inner", "outer"), -1
            )
            cached = None
        allowed = visible(
            seq_index,
            (seq_index - offset) % seq_count,
            offset,
            block_rows,
            sink_end,
            window,
            block_codes,
            seq_index - offset >= 0,
        )
        step_dq, step_dk, step_dv = backward_step(
            queries, out_grad, log_sum, row_delta, moving_k, moving_v, allowed, temper, cached
        )
        grad_q = grad_q + step_dq
        grad_keys = grad_keys + step_dk
        grad_values = grad_values + step_dv
    sink_dq, sink_dk, sink_dv = backward_step(
        queries, out_grad, log_sum, row_delta, sink_keys, sink_values, sink_allowed, temper, None
    )
    grad_q = grad_q + sink_dq
    total_dk, total_dv = lax.psum((sink_dk, sink_dv), ("inner", "outer"))
    is_first = seq_index == 0
    grad_keys = grad_keys.at[:SINK].add(jnp.where(is_first, total_dk, 0.0))
    grad_values = grad_values.at[:SINK].add(jnp.where(is_first, total_dv, 0.0))
    half_cols = key_rows.shape[1]
    keep_k = jnp.where(upper_half, grad_keys[:, half_cols:], grad_keys[:, :half_cols])
    send_k = jnp.where(upper_half, grad_keys[:, :half_cols], grad_keys[:, half_cols:])
    keep_v = jnp.where(upper_half, grad_values[:, half_cols:], grad_values[:, :half_cols])
    send_v = jnp.where(upper_half, grad_values[:, :half_cols], grad_values[:, half_cols:])
    got_k, got_v = swapped((send_k, send_v), "head", 0)
    return (grad_q, keep_k + got_k, keep_v + got_v)


def solution(mesh):
    in_specs = (
        P(("inner", "outer"), "head", None),
        P(("inner", "outer"), "head"),
        P(("inner", "outer"), "head"),
        P(("inner", "outer"), "head", None),
        P(),
        P(),
        P(),
    )
    out_specs = (
        P(("inner", "outer"), "head", None),
        P(("inner", "outer"), "head"),
        P(("inner", "outer"), "head"),
    )
    return jax.shard_map(shards, mesh=mesh, in_specs=in_specs, out_specs=out_specs, check_vma=False)
```

profile of v0, /device:TPU:0, one launch (start us, length us, event | category | flops | bytes accessed | tf_op | source)
XLA Modules:
  0.0 250.1 jit_solution(6072486249846511252)
XLA Ops:
  7.2 0.9 copy.10
  8.1 3.0 %collective-permute-start = (f32[128,64]{1,0:T(8,128)S(1)}, f32[128,64]{1,0:T(8,128)S(1)}, u32[]{:S(2)}, u32[]{:S(2)}) collective-permute-start(f32[128,64]{1,0:T(8,128)S(1)} %copy.10), channel_id=1, source_target_pairs={{0,16},{16,0},{1,17},{17,1},{2,18},{18,2},{3,19},{19,3},{4,20},{20... | collective-permute-start | bytes 98312 | tf_op jit(solution)/shard_map/ppermute | solution.py:17
  12.0 0.7 fusion.159
  21.8 0.7 broadcast_select_fusion.1
  22.5 2.1 collective-permute-start.1
  24.6 0.7 broadcast_select_fusion
  25.4 1.6 collective-permute-start.6
  27.4 1.5 collective-permute-done.1
  29.7 85.9 %all-reduce.7.cloned.1.call-done = (f32[128,128]{1,0:T(8,128)}, f32[128,128]{1,0:T(8,128)}) async-done(((f32[128,128]{1,0:T(8,128)}, f32[128,128]{1,0:T(8,128)}), (f32[128,128]{1,0:T(8,128)}, f32[128,128]{1,0:T(8,128)})) %all-reduce.7.cloned.1.call-update) | async-done | bytes 131088 | tf_op jit(solution)/shard_map/psum | solution.py:22
  115.6 1.2 select_reduce_fusion
  116.8 4.1 %collective-permute-start.7 = (f32[128,128]{1,0:T(8,128)S(1)}, f32[128,128]{1,0:T(8,128)S(1)}, u32[]{:S(2)}, u32[]{:S(2)}) collective-permute-start(f32[128,128]{1,0:T(8,128)S(1)} %collective-permute-done.6), channel_id=1, source_target_pairs={{0,1},{1,2},{2,3},{3,4},{4,5},{5,6},{6,7},{7,8},{8,9},{9,10},{10,1... | collective-permute-start | bytes 196616 | tf_op jit(solution)/shard_map/ppermute | solution.py:28
  121.4 1.8 collective-permute-done.7
  123.3 2.0 collective-permute-start.8
  125.2 2.1 collective-permute-done.3
  127.7 2.6 %collective-permute-done.8 = f32[128,128]{1,0:T(8,128)S(1)} collective-permute-done((f32[128,128]{1,0:T(8,128)S(1)}, f32[128,128]{1,0:T(8,128)S(1)}, u32[]{:S(2)}, u32[]{:S(2)}) %collective-permute-start.8) | collective-permute-done | bytes 65568 | tf_op jit(solution)/shard_map/ppermute | solution.py:28
  130.4 3.4 %collective-permute-done.4 = f32[128,128]{1,0:T(8,128)S(1)} collective-permute-done((f32[128,128]{1,0:T(8,128)S(1)}, f32[128,128]{1,0:T(8,128)S(1)}, u32[]{:S(2)}, u32[]{:S(2)}) %collective-permute-start.4) | collective-permute-done | bytes 65568 | tf_op jit(solution)/shard_map/ppermute | solution.py:28
  137.8 1.1 convolution_bitcast_fusion.6
  139.7 1.0 fusion.49
  141.2 1.1 collective-permute-start.23
  143.8 4.8 %collective-permute-done.10 = f32[128,128]{1,0:T(8,128)S(1)} collective-permute-done((f32[128,128]{1,0:T(8,128)S(1)}, f32[128,128]{1,0:T(8,128)S(1)}, u32[]{:S(2)}, u32[]{:S(2)}) %collective-permute-start.10) | collective-permute-done | bytes 65568 | tf_op jit(solution)/shard_map/ppermute | solution.py:28
  149.4 2.5 collective-permute-start.24
  153.7 5.5 %collective-permute-done.12 = f32[128,128]{1,0:T(8,128)S(1)} collective-permute-done((f32[128,128]{1,0:T(8,128)S(1)}, f32[128,128]{1,0:T(8,128)S(1)}, u32[]{:S(2)}, u32[]{:S(2)}) %collective-permute-start.12) | collective-permute-done | bytes 65568 | tf_op jit(solution)/shard_map/ppermute | solution.py:28
  160.1 1.9 collective-permute-start.25
  164.0 5.4 %collective-permute-done.14 = f32[128,128]{1,0:T(8,128)S(1)} collective-permute-done((f32[128,128]{1,0:T(8,128)S(1)}, f32[128,128]{1,0:T(8,128)S(1)}, u32[]{:S(2)}, u32[]{:S(2)}) %collective-permute-start.14) | collective-permute-done | bytes 65568 | tf_op jit(solution)/shard_map/ppermute | solution.py:28
  170.2 2.8 %collective-permute-start.26 = (f32[128,128]{1,0:T(8,128)S(1)}, f32[128,128]{1,0:T(8,128)S(1)}, u32[]{:S(2)}, u32[]{:S(2)}) collective-permute-start(f32[128,128]{1,0:T(8,128)S(1)} %add.358), channel_id=1, source_target_pairs={{0,15},{1,0},{2,1},{3,2},{4,3},{5,4},{6,5},{7,6},{8,7},{9,8},{10,9... | collective-permute-start | bytes 196616 | tf_op jit(solution)/shard_map/ppermute | solution.py:28
  174.7 4.6 %collective-permute-done.16 = f32[128,128]{1,0:T(8,128)S(1)} collective-permute-done((f32[128,128]{1,0:T(8,128)S(1)}, f32[128,128]{1,0:T(8,128)S(1)}, u32[]{:S(2)}, u32[]{:S(2)}) %collective-permute-start.16) | collective-permute-done | bytes 65568 | tf_op jit(solution)/shard_map/ppermute | solution.py:28
  180.1 54.2 %all-reduce.5.cloned.1.call-done = (f32[128,128]{1,0:T(8,128)}, f32[128,128]{1,0:T(8,128)}) async-done(((f32[128,128]{1,0:T(8,128)}, f32[128,128]{1,0:T(8,128)}), (f32[128,128]{1,0:T(8,128)}, f32[128,128]{1,0:T(8,128)})) %all-reduce.5.cloned.1.call-update) | async-done | bytes 131088 | tf_op jit(solution)/shard_map/psum | solution.py:166
  234.3 0.9 select_add_fusion.1
  235.2 1.5 collective-permute-start.27
  239.2 0.8 copy.78
  240.1 0.7 copy.80
  240.8 1.6 collective-permute-done.22
  (128 shorter events, 22.7 us)
Async XLA Ops:
  7.2 19.8 %copy-start = (f32[128,4,128]{2,1,0:T(4,128)S(1)}, f32[128,4,128]{2,1,0:T(4,128)}, u32[]{:S(2)}) copy-start(f32[128,4,128]{2,1,0:T(4,128)} %param.15) | copy-start | bytes 786436
  7.2 108.4 %all-reduce.7.cloned.1.call-start = ((), (), s32[]{:S(2)}) async-start(), calls=%async_computation.1 | async-start | bytes 262144 | tf_op jit(solution)/shard_map/psum | solution.py:22
  8.1 13.7 %collective-permute-start = (f32[128,64]{1,0:T(8,128)S(1)}, f32[128,64]{1,0:T(8,128)S(1)}, u32[]{:S(2)}, u32[]{:S(2)}) collective-permute-start(f32[128,64]{1,0:T(8,128)S(1)} %copy.10), channel_id=1, source_target_pairs={{0,16},{16,0},{1,17},{17,1},{2,18},{18,2},{3,19},{19,3},{4,20},{20... | collective-permute-start | bytes 98312 | tf_op jit(solution)/shard_map/ppermute | solution.py:17
  11.3 13.4 %collective-permute-start.5 = (f32[128,64]{1,0:T(8,128)S(1)}, f32[128,64]{1,0:T(8,128)S(1)}, u32[]{:S(2)}, u32[]{:S(2)}) collective-permute-start(f32[128,64]{1,0:T(8,128)S(1)} %copy.24), channel_id=1, source_target_pairs={{0,16},{16,0},{1,17},{17,1},{2,18},{18,2},{3,19},{19,3},{4,20},{20... | collective-permute-start | bytes 98312 | tf_op jit(solution)/shard_map/ppermute | solution.py:17
  11.4 10.3 %copy-start.1 = (f32[128,4,128]{2,1,0:T(4,128)S(1)}, f32[128,4,128]{2,1,0:T(4,128)}, u32[]{:S(2)}) copy-start(f32[128,4,128]{2,1,0:T(4,128)} %param.18) | copy-start | bytes 786436
  22.5 6.4 %collective-permute-start.1 = (f32[128,128]{1,0:T(8,128)S(1)}, f32[128,128]{1,0:T(8,128)S(1)}, u32[]{:S(2)}, u32[]{:S(2)}) collective-permute-start(f32[128,128]{1,0:T(8,128)S(1)} %get-tuple-element.80), channel_id=1, source_target_pairs={{0,1},{1,2},{2,3},{3,4},{4,5},{5,6},{6,7},{7,8},{8,9},{9,10},{10,1... | collective-permute-start | bytes 196616 | tf_op jit(solution)/shard_map/ppermute | solution.py:28
  25.4 91.5 %collective-permute-start.6 = (f32[128,128]{1,0:T(8,128)S(1)}, f32[128,128]{1,0:T(8,128)S(1)}, u32[]{:S(2)}, u32[]{:S(2)}) collective-permute-start(f32[128,128]{1,0:T(8,128)S(1)} %get-tuple-element.78), channel_id=1, source_target_pairs={{0,1},{1,2},{2,3},{3,4},{4,5},{5,6},{6,7},{7,8},{8,9},{9,10},{10,1... | collective-permute-start | bytes 196616 | tf_op jit(solution)/shard_map/ppermute | solution.py:28
  27.4 206.9 %all-reduce.5.cloned.1.call-start = ((), (), s32[]{:S(2)}) async-start(), calls=%async_computation | async-start | bytes 262144 | tf_op jit(solution)/shard_map/psum | solution.py:166
  28.9 92.0 %collective-permute-start.2 = (f32[128,128]{1,0:T(8,128)S(1)}, f32[128,128]{1,0:T(8,128)S(1)}, u32[]{:S(2)}, u32[]{:S(2)}) collective-permute-start(f32[128,128]{1,0:T(8,128)S(1)} %collective-permute-done.1), channel_id=1, source_target_pairs={{0,1},{1,2},{2,3},{3,4},{4,5},{5,6},{6,7},{7,8},{8,9},{9,10},{10,1... | collective-permute-start | bytes 196616 | tf_op jit(solution)/shard_map/ppermute | solution.py:28
  116.8 6.4 %collective-permute-start.7 = (f32[128,128]{1,0:T(8,128)S(1)}, f32[128,128]{1,0:T(8,128)S(1)}, u32[]{:S(2)}, u32[]{:S(2)}) collective-permute-start(f32[128,128]{1,0:T(8,128)S(1)} %collective-permute-done.6), channel_id=1, source_target_pairs={{0,1},{1,2},{2,3},{3,4},{4,5},{5,6},{6,7},{7,8},{8,9},{9,10},{10,1... | collective-permute-start | bytes 196616 | tf_op jit(solution)/shard_map/ppermute | solution.py:28
  121.0 6.4 %collective-permute-start.3 = (f32[128,128]{1,0:T(8,128)S(1)}, f32[128,128]{1,0:T(8,128)S(1)}, u32[]{:S(2)}, u32[]{:S(2)}) collective-permute-start(f32[128,128]{1,0:T(8,128)S(1)} %collective-permute-done.2), channel_id=1, source_target_pairs={{0,1},{1,2},{2,3},{3,4},{4,5},{5,6},{6,7},{7,8},{8,9},{9,10},{10,1... | collective-permute-start | bytes 196616 | tf_op jit(solution)/shard_map/ppermute | solution.py:28
  123.3 7.1 %collective-permute-start.8 = (f32[128,128]{1,0:T(8,128)S(1)}, f32[128,128]{1,0:T(8,128)S(1)}, u32[]{:S(2)}, u32[]{:S(2)}) collective-permute-start(f32[128,128]{1,0:T(8,128)S(1)} %collective-permute-done.7), channel_id=1, source_target_pairs={{0,1},{1,2},{2,3},{3,4},{4,5},{5,6},{6,7},{7,8},{8,9},{9,10},{10,1... | collective-permute-start | bytes 196616 | tf_op jit(solution)/shard_map/ppermute | solution.py:28
  127.3 6.4 %collective-permute-start.4 = (f32[128,128]{1,0:T(8,128)S(1)}, f32[128,128]{1,0:T(8,128)S(1)}, u32[]{:S(2)}, u32[]{:S(2)}) collective-permute-start(f32[128,128]{1,0:T(8,128)S(1)} %collective-permute-done.3), channel_id=1, source_target_pairs={{0,1},{1,2},{2,3},{3,4},{4,5},{5,6},{6,7},{7,8},{8,9},{9,10},{10,1... | collective-permute-start | bytes 196616 | tf_op jit(solution)/shard_map/ppermute | solution.py:28
  130.4 8.5 %collective-permute-start.9 = (f32[128,128]{1,0:T(8,128)S(1)}, f32[128,128]{1,0:T(8,128)S(1)}, u32[]{:S(2)}, u32[]{:S(2)}) collective-permute-start(f32[128,128]{1,0:T(8,128)S(1)} %collective-permute-done.8), channel_id=1, source_target_pairs={{0,1},{1,2},{2,3},{3,4},{4,5},{5,6},{6,7},{7,8},{8,9},{9,10},{10,1... | collective-permute-start | bytes 196616 | tf_op jit(solution)/shard_map/ppermute | solution.py:28
  141.2 7.8 %collective-permute-start.23 = (f32[128,128]{1,0:T(8,128)S(1)}, f32[128,128]{1,0:T(8,128)S(1)}, u32[]{:S(2)}, u32[]{:S(2)}) collective-permute-start(f32[128,128]{1,0:T(8,128)S(1)} %convolution_bitcast_fusion.11), channel_id=1, source_target_pairs={{0,15},{1,0},{2,1},{3,2},{4,3},{5,4},{6,5},{7,6},{8,7},{9,8},{10,9... | collective-permute-start | bytes 196616 | tf_op jit(solution)/shard_map/ppermute | solution.py:28
  143.1 9.1 %collective-permute-start.18 = (f32[128,128]{1,0:T(8,128)S(1)}, f32[128,128]{1,0:T(8,128)S(1)}, u32[]{:S(2)}, u32[]{:S(2)}) collective-permute-start(f32[128,128]{1,0:T(8,128)S(1)} %fusion.54), channel_id=1, source_target_pairs={{0,15},{1,0},{2,1},{3,2},{4,3},{5,4},{6,5},{7,6},{8,7},{9,8},{10,9... | collective-permute-start | bytes 196616 | tf_op jit(solution)/shard_map/ppermute | solution.py:28
  143.2 5.3 %collective-permute-start.10 = (f32[128,128]{1,0:T(8,128)S(1)}, f32[128,128]{1,0:T(8,128)S(1)}, u32[]{:S(2)}, u32[]{:S(2)}) collective-permute-start(f32[128,128]{1,0:T(8,128)S(1)} %collective-permute-done.4), channel_id=1, source_target_pairs={{0,15},{1,0},{2,1},{3,2},{4,3},{5,4},{6,5},{7,6},{8,7},{9,8},{10,9... | collective-permute-start | bytes 196616 | tf_op jit(solution)/shard_map/ppermute | solution.py:28
  143.3 8.6 %collective-permute-start.11 = (f32[128,128]{1,0:T(8,128)S(1)}, f32[128,128]{1,0:T(8,128)S(1)}, u32[]{:S(2)}, u32[]{:S(2)}) collective-permute-start(f32[128,128]{1,0:T(8,128)S(1)} %collective-permute-done.9), channel_id=1, source_target_pairs={{0,15},{1,0},{2,1},{3,2},{4,3},{5,4},{6,5},{7,6},{8,7},{9,8},{10,9... | collective-permute-start | bytes 196616 | tf_op jit(solution)/shard_map/ppermute | solution.py:28
  149.4 10.7 %collective-permute-start.24 = (f32[128,128]{1,0:T(8,128)S(1)}, f32[128,128]{1,0:T(8,128)S(1)}, u32[]{:S(2)}, u32[]{:S(2)}) collective-permute-start(f32[128,128]{1,0:T(8,128)S(1)} %fusion.56), channel_id=1, source_target_pairs={{0,15},{1,0},{2,1},{3,2},{4,3},{5,4},{6,5},{7,6},{8,7},{9,8},{10,9... | collective-permute-start | bytes 196616 | tf_op jit(solution)/shard_map/ppermute | solution.py:28
  152.7 10.2 %collective-permute-start.19 = (f32[128,128]{1,0:T(8,128)S(1)}, f32[128,128]{1,0:T(8,128)S(1)}, u32[]{:S(2)}, u32[]{:S(2)}) collective-permute-start(f32[128,128]{1,0:T(8,128)S(1)} %fusion.55), channel_id=1, source_target_pairs={{0,15},{1,0},{2,1},{3,2},{4,3},{5,4},{6,5},{7,6},{8,7},{9,8},{10,9... | collective-permute-start | bytes 196616 | tf_op jit(solution)/shard_map/ppermute | solution.py:28
  152.7 6.5 %collective-permute-start.12 = (f32[128,128]{1,0:T(8,128)S(1)}, f32[128,128]{1,0:T(8,128)S(1)}, u32[]{:S(2)}, u32[]{:S(2)}) collective-permute-start(f32[128,128]{1,0:T(8,128)S(1)} %collective-permute-done.10), channel_id=1, source_target_pairs={{0,15},{1,0},{2,1},{3,2},{4,3},{5,4},{6,5},{7,6},{8,7},{9,8},{10,9... | collective-permute-start | bytes 196616 | tf_op jit(solution)/shard_map/ppermute | solution.py:28
  152.8 9.2 %collective-permute-start.13 = (f32[128,128]{1,0:T(8,128)S(1)}, f32[128,128]{1,0:T(8,128)S(1)}, u32[]{:S(2)}, u32[]{:S(2)}) collective-permute-start(f32[128,128]{1,0:T(8,128)S(1)} %collective-permute-done.11), channel_id=1, source_target_pairs={{0,15},{1,0},{2,1},{3,2},{4,3},{5,4},{6,5},{7,6},{8,7},{9,8},{10,9... | collective-permute-start | bytes 196616 | tf_op jit(solution)/shard_map/ppermute | solution.py:28
  160.1 10.1 %collective-permute-start.25 = (f32[128,128]{1,0:T(8,128)S(1)}, f32[128,128]{1,0:T(8,128)S(1)}, u32[]{:S(2)}, u32[]{:S(2)}) collective-permute-start(f32[128,128]{1,0:T(8,128)S(1)} %add.357), channel_id=1, source_target_pairs={{0,15},{1,0},{2,1},{3,2},{4,3},{5,4},{6,5},{7,6},{8,7},{9,8},{10,9... | collective-permute-start | bytes 196616 | tf_op jit(solution)/shard_map/ppermute | solution.py:28
  162.9 11.0 %collective-permute-start.20 = (f32[128,128]{1,0:T(8,128)S(1)}, f32[128,128]{1,0:T(8,128)S(1)}, u32[]{:S(2)}, u32[]{:S(2)}) collective-permute-start(f32[128,128]{1,0:T(8,128)S(1)} %add.351), channel_id=1, source_target_pairs={{0,15},{1,0},{2,1},{3,2},{4,3},{5,4},{6,5},{7,6},{8,7},{9,8},{10,9... | collective-permute-start | bytes 196616 | tf_op jit(solution)/shard_map/ppermute | solution.py:28
  163.5 6.0 %collective-permute-start.14 = (f32[128,128]{1,0:T(8,128)S(1)}, f32[128,128]{1,0:T(8,128)S(1)}, u32[]{:S(2)}, u32[]{:S(2)}) collective-permute-start(f32[128,128]{1,0:T(8,128)S(1)} %collective-permute-done.12), channel_id=1, source_target_pairs={{0,15},{1,0},{2,1},{3,2},{4,3},{5,4},{6,5},{7,6},{8,7},{9,8},{10,9... | collective-permute-start | bytes 196616 | tf_op jit(solution)/shard_map/ppermute | solution.py:28
  163.5 9.5 %collective-permute-start.15 = (f32[128,128]{1,0:T(8,128)S(1)}, f32[128,128]{1,0:T(8,128)S(1)}, u32[]{:S(2)}, u32[]{:S(2)}) collective-permute-start(f32[128,128]{1,0:T(8,128)S(1)} %collective-permute-done.13), channel_id=1, source_target_pairs={{0,15},{1,0},{2,1},{3,2},{4,3},{5,4},{6,5},{7,6},{8,7},{9,8},{10,9... | collective-permute-start | bytes 196616 | tf_op jit(solution)/shard_map/ppermute | solution.py:28
  170.2 64.0 %collective-permute-start.26 = (f32[128,128]{1,0:T(8,128)S(1)}, f32[128,128]{1,0:T(8,128)S(1)}, u32[]{:S(2)}, u32[]{:S(2)}) collective-permute-start(f32[128,128]{1,0:T(8,128)S(1)} %add.358), channel_id=1, source_target_pairs={{0,15},{1,0},{2,1},{3,2},{4,3},{5,4},{6,5},{7,6},{8,7},{9,8},{10,9... | collective-permute-start | bytes 196616 | tf_op jit(solution)/shard_map/ppermute | solution.py:28
  173.8 63.7 %collective-permute-start.21 = (f32[128,128]{1,0:T(8,128)S(1)}, f32[128,128]{1,0:T(8,128)S(1)}, u32[]{:S(2)}, u32[]{:S(2)}) collective-permute-start(f32[128,128]{1,0:T(8,128)S(1)} %add.352), channel_id=1, source_target_pairs={{0,15},{1,0},{2,1},{3,2},{4,3},{5,4},{6,5},{7,6},{8,7},{9,8},{10,9... | collective-permute-start | bytes 196616 | tf_op jit(solution)/shard_map/ppermute | solution.py:28
  174.1 5.2 %collective-permute-start.16 = (f32[128,128]{1,0:T(8,128)S(1)}, f32[128,128]{1,0:T(8,128)S(1)}, u32[]{:S(2)}, u32[]{:S(2)}) collective-permute-start(f32[128,128]{1,0:T(8,128)S(1)} %collective-permute-done.14), channel_id=1, source_target_pairs={{0,15},{1,0},{2,1},{3,2},{4,3},{5,4},{6,5},{7,6},{8,7},{9,8},{10,9... | collective-permute-start | bytes 196616 | tf_op jit(solution)/shard_map/ppermute | solution.py:28
  174.2 62.6 %collective-permute-start.17 = (f32[128,128]{1,0:T(8,128)S(1)}, f32[128,128]{1,0:T(8,128)S(1)}, u32[]{:S(2)}, u32[]{:S(2)}) collective-permute-start(f32[128,128]{1,0:T(8,128)S(1)} %collective-permute-done.15), channel_id=1, source_target_pairs={{0,15},{1,0},{2,1},{3,2},{4,3},{5,4},{6,5},{7,6},{8,7},{9,8},{10,9... | collective-permute-start | bytes 196616 | tf_op jit(solution)/shard_map/ppermute | solution.py:28
  235.2 4.8 %collective-permute-start.27 = (f32[128,64]{1,0:T(8,128)S(1)}, f32[128,64]{1,0:T(8,128)S(1)}, u32[]{:S(2)}, u32[]{:S(2)}) collective-permute-start(f32[128,64]{1,0:T(8,128)S(1)} %slice_select_fusion), channel_id=1, source_target_pairs={{0,16},{16,0},{1,17},{17,1},{2,18},{18,2},{3,19},{19,3},{4,20},{20... | collective-permute-start | bytes 98312 | tf_op jit(solution)/shard_map/ppermute | solution.py:17
  238.1 4.3 %collective-permute-start.22 = (f32[128,64]{1,0:T(8,128)S(1)}, f32[128,64]{1,0:T(8,128)S(1)}, u32[]{:S(2)}, u32[]{:S(2)}) collective-permute-start(f32[128,64]{1,0:T(8,128)S(1)} %slice_select_fusion.1), channel_id=1, source_target_pairs={{0,16},{16,0},{1,17},{17,1},{2,18},{18,2},{3,19},{19,3},{4,20},{20... | collective-permute-start | bytes 98312 | tf_op jit(solution)/shard_map/ppermute | solution.py:17
  (5 other events, 7.4 us)
Sparse Core Ops, SparseCore 0:
  27.5 88.0 all-reduce.6
  143.3 90.9 all-reduce.4
where the time goes:
time: 251 us; the launch traced here: 250 us
  waiting for transfers between devices  174 us (69%)
  starting transfers between devices  25.9 us (10%)
  between operations  22.5 us (9%)
  matrix products  18.3 us (7%)
  local copies, waits for them, and re-layouts  5.42 us (2%)
  other arithmetic  4.38 us (2%)
    psum x1, waiting for transfers between devices, spread(): return lax.psum(jnp.where(mine, array, jnp.zeros_like(array)), axis)  85.9 us
    psum x1, waiting for transfers between devices, shards(): total_dk, total_dv = lax.psum((sink_dk, sink_dv), ('inner', 'outer'))  54.2 us
    ppermute x24, waiting for transfers between devices, shifted(): return lax.ppermute(value, axis, pairs)  31.8 us
    ppermute x24, starting transfers between devices, shifted(): return lax.ppermute(value, axis, pairs)  20.5 us
    ppermute x4, starting transfers between devices, swapped(): lax.ppermute(array, axis, [(i, i ^ 1 << distance) for i in range(lax.axis...  5.28 us
  transfers between devices with their start and end apart: 30, of which 12 were waited for; matrix products, arithmetic and copies ran while one was open for 9% of the time, Pallas kernels for 0%

commit v1 on v0

v1 whole, which is shorter than its diff:
```python
import functools
import math

import jax
import jax.numpy as jnp
from jax import lax
from jax.experimental import pallas as pl
from jax.experimental.pallas import tpu as pltpu
from jax.sharding import PartitionSpec as P

STEPS = 5
FAR = STEPS - 1
BIG = 1 << 28
very_low = -1e30
f32, bf16 = jnp.float32, jnp.bfloat16
MESH = pl.DeviceIdType.MESH
NT = (((1,), (1,)), ((), ()))
NN = (((1,), (0,)), ((), ()))


def dot(a, b, dims):
    return lax.dot_general(a, b, dims, preferred_element_type=f32)


def two(x):
    hi = x.astype(bf16)
    return hi, (x - hi.astype(f32)).astype(bf16)


def three(x):
    hi = x.astype(bf16)
    rest = x - hi.astype(f32)
    mid = rest.astype(bf16)
    return hi, mid, (rest - mid.astype(f32)).astype(bf16)


def kernel(
    sizes, sink_ref, window_ref, codes_ref, q_ref, k_ref, v_ref, g_ref, dq_ref, dk_ref, dv_ref,
    buf, sinkb, piece, qcat, gcat, st, dp, dshi, dslo, ktcat,
    xout, xin, mine, gout, gin, g4out, g4in, sg, sin, s2, s2in, s3, s3in, send, recv,
):
    ni, no, heads_dev = sizes
    block, half = k_ref.shape
    rows = q_ref.shape[0]
    temper = 1.0 / math.sqrt(2 * half)
    head, inner, outer = lax.axis_index("head"), lax.axis_index("inner"), lax.axis_index("outer")
    par = lax.rem(head, 2)
    other = 1 - par
    partner = head + 1 - 2 * par
    count = ni * no
    b = inner * no + outer
    pr = block // ni

    def seq(o):
        t = lax.rem(b + o + count, count)
        return (head, t // no, lax.rem(t, no))

    across = (partner, inner, outer)
    columns = [(p, d) for p in range(2) for d in range(ni) if p or d]

    def column(p, d):
        return (partner if p else head, lax.rem(inner + d, ni), outer)

    def source(d):
        return lax.rem(inner - d + ni, ni)

    slots = {}

    def sem(name):
        return slots.setdefault(name, len(slots))

    pending = []

    def copy(name, src, dst, device):
        k = sem(name)
        return pltpu.make_async_remote_copy(
            src_ref=src, dst_ref=dst, send_sem=send.at[k], recv_sem=recv.at[k],
            device_id=device, device_id_type=MESH,
        )

    def start(name, src, dst, device):
        c = copy(name, src, dst, device)
        c.start()
        pending.append(c)

    def arrived(name, dst):
        copy(name, dst, dst, across).wait_recv()

    buf[0, par, :, 0:half] = k_ref[...]
    buf[0, par, :, half:2 * half] = v_ref[...]

    barrier = pltpu.get_barrier_semaphore()
    greet = [seq(s * o) for o in range(1, STEPS) for s in (1, -1)]
    greet += [column(p, d) for p, d in columns]
    greet += [(head, inner, lax.rem(outer + d, no)) for d in range(1, no)]
    for device in greet:
        pl.semaphore_signal(barrier, inc=1, device_id=device, device_id_type=MESH)

    q0, q1, q2 = three(q_ref[...])
    qcat[...] = jnp.concatenate([q0, q1, q0, q1, q2, q0], 1)
    g0, g1, g2 = three(g_ref[...])
    gcat[...] = jnp.concatenate([g0, g1, g0, g1, g2, g0], 1)
    pl.semaphore_wait(barrier, len(greet))

    own = buf.at[0, par]
    first = (inner == 0) & (outer == 0)
    top = outer == 0
    at_root = piece

    @pl.when(first)
    def _():
        for i in range(1, ni):
            copy(f"f1_{i}", own.at[pl.ds(i * pr, pr)], at_root, (head, i, outer)).start()
        piece[...] = buf[0, par, 0:pr, :]

    start("x0", own, own, across)
    for o in range(FAR, 0, -1):
        start(f"w{o}", own, buf.at[o, par], seq(o))

    def scores_of(a, c, index, allowed):
        lane = lax.broadcasted_iota(jnp.int32, (block, 2 * half), 1)
        low = lane < half
        keys = jnp.where(low, a, pltpu.roll(c, half, 1))
        vals = jnp.where(low, pltpu.roll(a, half, 1), c)
        k0, k1, k2 = three(keys)
        v0, v1, v2 = three(vals)
        s = dot(jnp.concatenate([k0, k0, k1, k1, k0, k2], 1), qcat[...], NT)
        st[index] = jnp.where(allowed, temper * s, very_low)
        dp[index] = dot(jnp.concatenate([v0, v0, v1, v1, v0, v2], 1), gcat[...], NT)
        t0, t1 = two(keys.T * temper)
        ktcat[index] = jnp.concatenate([t0, t1, t0], 1)

    jk = lax.broadcasted_iota(jnp.int32, (block, rows), 0)
    iq = lax.broadcasted_iota(jnp.int32, (block, rows), 1) // heads_dev
    gap = iq - jk
    sink_end, window = sink_ref[0], window_ref[0]

    def mask_of(o):
        code = codes_ref[b, o]
        limit = jnp.where(code == 2, BIG, jnp.where(code == 1, window, -BIG))
        limit = jnp.where(b >= o, limit, -BIG) - o * block
        here = jnp.where(b == o, sink_end, 0)
        if o == 0:
            return (gap >= 0) & ((gap < limit) | (jk < here))
        return (gap < limit) & (jk >= here)

    def slot(o):
        scores_of(buf[o, 0], buf[o, 1], o, mask_of(o))

    arrived("x0", buf.at[0, other])
    start("w4x", buf.at[0, other], buf.at[FAR, other], seq(FAR))

    @pl.when(top)
    def _():
        @pl.when(inner != 0)
        def _():
            for i in range(1, ni):
                @pl.when(inner == i)
                def _():
                    arrived(f"f1_{i}", piece)
        for z in range(1, no):
            copy(f"f2_{z}", piece, piece, (head, inner, z)).start()

    slot(0)
    for o in range(1, FAR):
        arrived(f"w{o}", buf.at[o, par])
        start(f"r{o}", buf.at[o, par], buf.at[o, par], across)

    @pl.when(outer != 0)
    def _():
        for z in range(1, no):
            @pl.when(outer == z)
            def _():
                arrived(f"f2_{z}", piece)

    where = pl.ds(pl.multiple_of(inner * pr, pr), pr)
    for p, d in columns:
        start(f"f3_{p}_{d}", piece, sinkb.at[par, where], column(p, d))
    sinkb[par, where] = piece[...]

    arrived(f"w{FAR}", buf.at[FAR, par])
    arrived("w4x", buf.at[FAR, other])
    slot(FAR)
    for o in range(1, FAR):
        arrived(f"r{o}", buf.at[o, other])
        slot(o)
    for p, d in columns:
        there = pl.ds(pl.multiple_of(source(d) * pr, pr), pr)
        arrived(f"f3_{p}_{d}", sinkb.at[other if p else par, there])
    scores_of(sinkb[0], sinkb[1], STEPS, jk < jnp.where(b >= 1, sink_end, 0))

    total = STEPS + 1
    top_score = jnp.max(st[0], axis=0, keepdims=True)
    for i in range(1, total):
        top_score = jnp.maximum(top_score, jnp.max(st[i], axis=0, keepdims=True))
    norm = jnp.zeros((1, rows), f32)
    delta = jnp.zeros((1, rows), f32)
    for i in range(total):
        e = jnp.exp(st[i] - top_score)
        st[i] = e
        norm = norm + jnp.sum(e, axis=0, keepdims=True)
        delta = delta + jnp.sum(e * dp[i], axis=0, keepdims=True)
    scale = 1.0 / norm
    delta = delta * scale

    def grads(i):
        probs = st[i] * scale
        ds = probs * (dp[i] - delta)
        p_hi, p_lo = two(probs)
        d_hi, d_lo = two(ds)
        dshi[i] = d_hi
        dslo[i] = d_lo
        w = 2 * half
        pv = dot(p_hi, gcat[:, 0:2 * w], NN)
        dv = pv[:, 0:w] + pv[:, w:] + dot(p_lo, gcat[:, 0:w], NN)
        kq = dot(d_hi, qcat[:, 0:2 * w], NN)
        dk = temper * (kq[:, 0:w] + kq[:, w:] + dot(d_lo, qcat[:, 0:w], NN))
        low = lax.broadcasted_iota(jnp.int32, (block, w), 1) < half
        even = jnp.where(low, dk, pltpu.roll(dv, half, 1))
        odd = jnp.where(low, pltpu.roll(dk, half, 1), dv)
        keep = jnp.where(par == 0, even, odd)
        give = jnp.where(par == 0, odd, even)
        return keep, give

    keep, give = grads(STEPS)
    sg[0] = keep
    sg[1] = give
    for p, d in columns:
        target = lax.rem(inner + d, ni)
        rng = pl.ds(pl.multiple_of(target * pr, pr), pr)
        start(f"b1_{p}_{d}", sg.at[p, rng], sin.at[p * ni + d], column(p, d))

    keep, give = grads(FAR)
    g4out[0] = keep
    g4out[1] = give
    start("g4k", g4out.at[0], g4in.at[0], seq(-FAR))
    start("g4g", g4out.at[1], g4in.at[1], seq(-FAR))

    def pass_on(o):
        arrived(f"gx{o}", xin.at[o])
        gout[o] = mine[o] + xin[o]
        start(f"gz{o}", gout.at[o], gin.at[o], seq(-o))

    for o in range(FAR - 1, 0, -1):
        keep, give = grads(o)
        mine[o] = keep
        xout[o] = give
        start(f"gx{o}", xout.at[o], xin.at[o], across)
        if o < FAR - 1:
            pass_on(o + 1)
    keep, give = grads(0)
    arrived("g4g", g4in.at[1])
    xout[0] = give + g4in[1]
    start("gx0", xout.at[0], xin.at[0], across)
    pass_on(1)
    arrived("g4k", g4in.at[0])
    mine[0] = keep + g4in[0]

    for p, d in columns:
        arrived(f"b1_{p}_{d}", sin.at[p * ni + d])
    acc = sg[0, where]
    for p, d in columns:
        acc = acc + sin[p * ni + d]
    s2[...] = acc
    for z in range(1, no):
        @pl.when(outer == z)
        def _():
            copy(f"b2_{z}", s2, s2in.at[z], (head, inner, 0)).start()

    dqt = jnp.zeros((2 * half, rows), f32)
    for i in range(total):
        hi = dshi[i]
        dqt = dqt + dot(ktcat[i], jnp.concatenate([hi, hi, dslo[i]], 0), NN)
    dq_ref[...] = dqt.T

    @pl.when(top)
    def _():
        part = s2[...]
        for z in range(1, no):
            arrived(f"b2_{z}", s2in.at[z])
            part = part + s2in[z]
        s3[...] = part
        for i in range(1, ni):
            @pl.when(inner == i)
            def _():
                copy(f"b3_{i}", s3, s3in.at[i], (head, 0, outer)).start()

    arrived("gx0", xin.at[0])
    acc = mine[0] + xin[0]
    for o in range(FAR - 1, 0, -1):
        arrived(f"gz{o}", gin.at[o])
        acc = acc + gin[o]
    mine[0] = acc

    @pl.when(first)
    def _():
        mine[0, 0:pr] += s3[...]
        for i in range(1, ni):
            arrived(f"b3_{i}", s3in.at[i])
            mine[0, i * pr:(i + 1) * pr] += s3in[i]

    acc = mine[0]
    dk_ref[...] = acc[:, 0:half]
    dv_ref[...] = acc[:, half:]

    for c in pending:
        c.wait_send()

    @pl.when(first)
    def _():
        for i in range(1, ni):
            copy(f"f1_{i}", own.at[pl.ds(i * pr, pr)], at_root, (head, i, outer)).wait_send()

    @pl.when(top)
    def _():
        for z in range(1, no):
            copy(f"f2_{z}", piece, piece, (head, inner, z)).wait_send()
        for i in range(1, ni):
            @pl.when(inner == i)
            def _():
                copy(f"b3_{i}", s3, s3in.at[i], (head, 0, outer)).wait_send()

    for z in range(1, no):
        @pl.when(outer == z)
        def _():
            copy(f"b2_{z}", s2, s2in.at[z], (head, inner, 0)).wait_send()
    assert len(slots) <= send.shape[0]


def shards(ni, no, queries, key_rows, values, out_grad, sink_len, window_len, block_codes):
    block, heads_dev, dim = queries.shape
    rows = block * heads_dev
    half = key_rows.shape[1]
    pr = block // ni
    total = STEPS + 1
    sems = 2 * (ni - 1) + 2 * (no - 1) + 2 * (2 * ni - 1) + 4 * STEPS
    vmem, smem = pl.BlockSpec(memory_space=pltpu.VMEM), pl.BlockSpec(memory_space=pltpu.SMEM)
    tile = (block, dim)
    grad_q, grad_k, grad_v = pl.pallas_call(
        functools.partial(kernel, (ni, no, heads_dev)),
        out_shape=(
            jax.ShapeDtypeStruct((rows, dim), f32),
            jax.ShapeDtypeStruct((block, half), f32),
            jax.ShapeDtypeStruct((block, half), f32),
        ),
        in_specs=[smem] * 3 + [vmem] * 4,
        out_specs=(vmem,) * 3,
        scratch_shapes=[
            pltpu.VMEM((STEPS, 2) + tile, f32),
            pltpu.VMEM((2,) + tile, f32),
            pltpu.VMEM((pr, dim), f32),
            pltpu.VMEM((rows, 6 * dim), bf16),
            pltpu.VMEM((rows, 6 * dim), bf16),
            pltpu.VMEM((total, block, rows), f32),
            pltpu.VMEM((total, block, rows), f32),
            pltpu.VMEM((total, block, rows), bf16),
            pltpu.VMEM((total, block, rows), bf16),
            pltpu.VMEM((total, dim, 3 * block), bf16),
            pltpu.VMEM((FAR,) + tile, f32),
            pltpu.VMEM((FAR,) + tile, f32),
            pltpu.VMEM((FAR,) + tile, f32),
            pltpu.VMEM((FAR,) + tile, f32),
            pltpu.VMEM((FAR,) + tile, f32),
            pltpu.VMEM((2,) + tile, f32),
            pltpu.VMEM((2,) + tile, f32),
            pltpu.VMEM((2,) + tile, f32),
            pltpu.VMEM((2 * ni, pr, dim), f32),
            pltpu.VMEM((pr, dim), f32),
            pltpu.VMEM((no, pr, dim), f32),
            pltpu.VMEM((pr, dim), f32),
            pltpu.VMEM((ni, pr, dim), f32),
            pltpu.SemaphoreType.DMA((sems,)),
            pltpu.SemaphoreType.DMA((sems,)),
        ],
        compiler_params=pltpu.CompilerParams(
            collective_id=0, has_side_effects=True, vmem_limit_bytes=48 << 20
        ),
    )(
        sink_len, window_len, block_codes,
        queries.reshape(rows, dim), key_rows, values, out_grad.reshape(rows, dim),
    )
    return grad_q.reshape(queries.shape), grad_k, grad_v


def solution(mesh):
    in_specs = (
        P(("inner", "outer"), "head", None),
        P(("inner", "outer"), "head"),
        P(("inner", "outer"), "head"),
        P(("inner", "outer"), "head", None),
        P(),
        P(),
        P(),
    )
    out_specs = (
        P(("inner", "outer"), "head", None),
        P(("inner", "outer"), "head"),
        P(("inner", "outer"), "head"),
    )
    body = functools.partial(shards, mesh.shape["inner"], mesh.shape["outer"])
    return jax.shard_map(body, mesh=mesh, in_specs=in_specs, out_specs=out_specs, check_vma=False)
```

time: 251 us -> 46 us (0.18)
  waiting for transfers between devices: 174 us -> 0 us
  Pallas kernels: 0 us -> 38.7 us
  starting transfers between devices: 25.9 us -> 0 us
  between operations: 22.5 us -> 1.99 us
  matrix products: 18.3 us -> 0 us
  other arithmetic: 4.38 us -> 0 us
    psum x2 -> x0, waiting for transfers between devices: 140 us -> none  [the longest x1 85.9 us: spread(): return lax.psum(jnp.where(mine, array, jnp.zeros_like(array)), axis)]
    pallas_call x0 -> x1, Pallas kernels: none -> 38.7 us  [shards(): pl.pallas_call(functools.partial(kernel, (ni, no, heads_dev)), out_shape=...]
    ppermute x28 -> x0, waiting for transfers between devices: 33.5 us -> none  [the longest x24 31.8 us: shifted(): return lax.ppermute(value, axis, pairs)]
    ppermute x28 -> x0, starting transfers between devices: 25.8 us -> none  [the longest x24 20.5 us: shifted(): return lax.ppermute(value, axis, pairs)]
    dot_general x40 -> x0, matrix products: 18.3 us -> none  [the longest x10 4.86 us: scores(): jnp.einsum('qhd,kd->hqk', query_blk, key_blk, precision=precise)]
    unnamed x20 -> x14, local copies, waits for them, and re-layouts: 4.82 us -> 5.03 us
  transfers between devices with their start and end apart: 30 -> 0, of which waited for: 12 -> 0; matrix products, arithmetic and copies ran while one was open for 9% -> 0% of each run, Pallas kernels for 0% -> 0%
where the time goes in v1:
time: 46 us; the launch traced here: 45.7 us
  Pallas kernels  38.7 us (84%)
  local copies, waits for them, and re-layouts  5.03 us (11%)
  between operations  1.99 us (4%)
    pallas_call x1, Pallas kernels, shards(): pl.pallas_call(functools.partial(kernel, (ni, no, heads_dev)), out_shape=...  38.7 us
    unnamed x14, local copies, waits for them, and re-layouts  5.03 us

profile of v1, /device:TPU:0, one launch (start us, length us, event | category | flops | bytes accessed | tf_op | source)
XLA Modules:
  0.0 45.7 jit_solution(9296192010868183453)
XLA Ops:
  0.6 0.0 copy-start.3
  1.9 0.0 copy-done.3
  2.0 0.1 copy.10.codes_ref
  2.0 0.0 copy-start.2
  2.0 0.9 %copy.11.k_ref = f32[128,64]{1,0:T(8,128)S(1)} copy(f32[128,64]{0,1:T(8,128)} %param.8) | data formatting | bytes 65536 | tf_op args[1]
  2.9 0.0 copy-done.2
  2.9 0.1 copy.12.v_ref
  3.0 0.0 copy-start
  3.0 0.9 %copy-done = f32[128,4,128]{2,1,0:T(4,128)S(1)} copy-done((f32[128,4,128]{2,1,0:T(4,128)S(1)}, f32[128,4,128]{2,1,0:T(4,128)}, u32[]{:S(2)}) %copy-start) | copy-done | bytes 262168
  4.0 0.0 copy-start.1
  4.0 0.9 %copy-done.1 = f32[128,4,128]{2,1,0:T(4,128)S(1)} copy-done((f32[128,4,128]{2,1,0:T(4,128)S(1)}, f32[128,4,128]{2,1,0:T(4,128)}, u32[]{:S(2)}) %copy-start.1) | copy-done | bytes 262168
  4.9 38.7 %shard_map.94 = (f32[512,128]{1,0:T(8,128)S(1)}, f32[128,64]{1,0:T(8,128)S(1)}, f32[128,64]{1,0:T(8,128)S(1)}) custom-call(s32[1]{0:T(128)S(6)} %copy.16.sink_ref, s32[1]{0:T(128)S(6)} %copy.17.window_ref, s32[16,5]{1,0:T(8,128)S(1)} %copy.10.codes_ref, f32[512,128]{1,0:T(8,128)S(1)} %bitcast.3, f32[128,64]{1,0:T(8,128)S(1)} %copy.11.k_ref, ...), custom_call_target="tpu_custom_call" | custom-call | tf_op jit(solution)/shard_map/pallas_call | solution.py:339
  43.6 0.7 %copy.13 = f32[128,64]{0,1:T(8,128)} copy(f32[128,64]{1,0:T(8,128)S(1)} %get-tuple-element.10) | data formatting | bytes 65536
  44.3 0.7 %copy.14 = f32[128,64]{0,1:T(8,128)} copy(f32[128,64]{1,0:T(8,128)S(1)} %get-tuple-element.11) | data formatting | bytes 65536
  45.0 0.7 %copy.18 = f32[128,4,128]{2,1,0:T(4,128)} copy(f32[128,4,128]{2,1,0:T(4,128)S(1)} %bitcast.5) | data formatting | bytes 524288
Async XLA Ops:
  0.6 1.3 %copy-start.3 = (s32[16,5]{0,1:T(8,128)S(1)}, s32[16,5]{0,1:T(8,128)}, u32[]{:S(2)}) copy-start(s32[16,5]{0,1:T(8,128)} %param.13) | copy-start | bytes 964
  2.0 0.9 %copy-start.2 = (f32[128,64]{0,1:T(8,128)S(1)}, f32[128,64]{0,1:T(8,128)}, u32[]{:S(2)}) copy-start(f32[128,64]{0,1:T(8,128)} %param.9) | copy-start | bytes 98308
  3.0 1.0 %copy-start = (f32[128,4,128]{2,1,0:T(4,128)S(1)}, f32[128,4,128]{2,1,0:T(4,128)}, u32[]{:S(2)}) copy-start(f32[128,4,128]{2,1,0:T(4,128)} %param.7) | copy-start | bytes 786436
  4.0 0.9 %copy-start.1 = (f32[128,4,128]{2,1,0:T(4,128)S(1)}, f32[128,4,128]{2,1,0:T(4,128)}, u32[]{:S(2)}) copy-start(f32[128,4,128]{2,1,0:T(4,128)} %param.10) | copy-start | bytes 786436

commit v2 on v1

--- a/solution.py
+++ b/solution.py
@@ -35,12 +35,12 @@
 
 
 def kernel(
-    sizes, sink_ref, window_ref, codes_ref, q_ref, k_ref, v_ref, g_ref, dq_ref, dk_ref, dv_ref,
-    buf, sinkb, piece, qcat, gcat, st, dp, dshi, dslo, ktcat,
+    sizes, sink_ref, window_ref, codes_hbm, q_hbm, k_hbm, v_hbm, g_hbm, dq_ref, dkv_ref,
+    codes_ref, q_ref, g_ref, load, buf, sinkb, piece, qcat, gcat, st, dp, dshi, dslo, ktcat,
     xout, xin, mine, gout, gin, g4out, g4in, sg, sin, s2, s2in, s3, s3in, send, recv,
 ):
     ni, no, heads_dev = sizes
-    block, half = k_ref.shape
+    half, block = k_hbm.shape
     rows = q_ref.shape[0]
     temper = 1.0 / math.sqrt(2 * half)
     head, inner, outer = lax.axis_index("head"), lax.axis_index("inner"), lax.axis_index("outer")
@@ -86,8 +86,14 @@
     def arrived(name, dst):
         copy(name, dst, dst, across).wait_recv()
 
-    buf[0, par, :, 0:half] = k_ref[...]
-    buf[0, par, :, half:2 * half] = v_ref[...]
+    moves = [
+        (k_hbm, buf.at[0, par, 0:half]), (v_hbm, buf.at[0, par, half:2 * half]),
+        (q_hbm, q_ref), (g_hbm, g_ref),
+        (codes_hbm, codes_ref),
+    ]
+    loads = [pltpu.make_async_copy(x, y, load.at[i]) for i, (x, y) in enumerate(moves)]
+    for x in loads:
+        x.start()
 
     barrier = pltpu.get_barrier_semaphore()
     greet = [seq(s * o) for o in range(1, STEPS) for s in (1, -1)]
@@ -96,6 +102,8 @@
     for device in greet:
         pl.semaphore_signal(barrier, inc=1, device_id=device, device_id_type=MESH)
 
+    for x in loads:
+        x.wait()
     q0, q1, q2 = three(q_ref[...])
     qcat[...] = jnp.concatenate([q0, q1, q0, q1, q2, q0], 1)
     g0, g1, g2 = three(g_ref[...])
@@ -118,16 +126,14 @@
         start(f"w{o}", own, buf.at[o, par], seq(o))
 
     def scores_of(a, c, index, allowed):
-        lane = lax.broadcasted_iota(jnp.int32, (block, 2 * half), 1)
-        low = lane < half
-        keys = jnp.where(low, a, pltpu.roll(c, half, 1))
-        vals = jnp.where(low, pltpu.roll(a, half, 1), c)
-        k0, k1, k2 = three(keys)
-        v0, v1, v2 = three(vals)
+        keys = jnp.concatenate([a[0:half], c[0:half]], 0)
+        vals = jnp.concatenate([a[half:], c[half:]], 0)
+        k0, k1, k2 = three(keys.T)
+        v0, v1, v2 = three(vals.T)
         s = dot(jnp.concatenate([k0, k0, k1, k1, k0, k2], 1), qcat[...], NT)
         st[index] = jnp.where(allowed, temper * s, very_low)
         dp[index] = dot(jnp.concatenate([v0, v0, v1, v1, v0, v2], 1), gcat[...], NT)
-        t0, t1 = two(keys.T * temper)
+        t0, t1 = two(keys * temper)
         ktcat[index] = jnp.concatenate([t0, t1, t0], 1)
 
     jk = lax.broadcasted_iota(jnp.int32, (block, rows), 0)
@@ -136,7 +142,7 @@
     sink_end, window = sink_ref[0], window_ref[0]
 
     def mask_of(o):
-        code = codes_ref[b, o]
+        code = codes_ref[o, b]
         limit = jnp.where(code == 2, BIG, jnp.where(code == 1, window, -BIG))
         limit = jnp.where(b >= o, limit, -BIG) - o * block
         here = jnp.where(b == o, sink_end, 0)
@@ -215,9 +221,9 @@
         dv = pv[:, 0:w] + pv[:, w:] + dot(p_lo, gcat[:, 0:w], NN)
         kq = dot(d_hi, qcat[:, 0:2 * w], NN)
         dk = temper * (kq[:, 0:w] + kq[:, w:] + dot(d_lo, qcat[:, 0:w], NN))
-        low = lax.broadcasted_iota(jnp.int32, (block, w), 1) < half
-        even = jnp.where(low, dk, pltpu.roll(dv, half, 1))
-        odd = jnp.where(low, pltpu.roll(dk, half, 1), dv)
+        dk, dv = dk.T, dv.T
+        even = jnp.concatenate([dk[0:half], dv[0:half]], 0)
+        odd = jnp.concatenate([dk[half:], dv[half:]], 0)
         keep = jnp.where(par == 0, even, odd)
         give = jnp.where(par == 0, odd, even)
         return keep, give
@@ -248,14 +254,6 @@
         start(f"gx{o}", xout.at[o], xin.at[o], across)
         if o < FAR - 1:
             pass_on(o + 1)
-    keep, give = grads(0)
-    arrived("g4g", g4in.at[1])
-    xout[0] = give + g4in[1]
-    start("gx0", xout.at[0], xin.at[0], across)
-    pass_on(1)
-    arrived("g4k", g4in.at[0])
-    mine[0] = keep + g4in[0]
-
     for p, d in columns:
         arrived(f"b1_{p}_{d}", sin.at[p * ni + d])
     acc = sg[0, where]
@@ -267,6 +265,14 @@
         def _():
             copy(f"b2_{z}", s2, s2in.at[z], (head, inner, 0)).start()
 
+    keep, give = grads(0)
+    arrived("g4g", g4in.at[1])
+    xout[0] = give + g4in[1]
+    start("gx0", xout.at[0], xin.at[0], across)
+    pass_on(1)
+    arrived("g4k", g4in.at[0])
+    mine[0] = keep + g4in[0]
+
     dqt = jnp.zeros((2 * half, rows), f32)
     for i in range(total):
         hi = dshi[i]
@@ -299,9 +305,7 @@
             arrived(f"b3_{i}", s3in.at[i])
             mine[0, i * pr:(i + 1) * pr] += s3in[i]
 
-    acc = mine[0]
-    dk_ref[...] = acc[:, 0:half]
-    dv_ref[...] = acc[:, half:]
+    dkv_ref[...] = mine[0]
 
     for c in pending:
         c.wait_send()
@@ -327,25 +331,42 @@
     assert len(slots) <= send.shape[0]
 
 
+def store(dq_ref, dkv_ref, dq_hbm, dk_hbm, dv_hbm, sem):
+    half = dk_hbm.shape[0]
+    moves = [
+        (dq_ref, dq_hbm), (dkv_ref.at[0:half], dk_hbm), (dkv_ref.at[half:2 * half], dv_hbm),
+    ]
+    copies = [pltpu.make_async_copy(x, y, sem.at[i]) for i, (x, y) in enumerate(moves)]
+    for c in copies:
+        c.start()
+    for c in copies:
+        c.wait()
+
+
 def shards(ni, no, queries, key_rows, values, out_grad, sink_len, window_len, block_codes):
     block, heads_dev, dim = queries.shape
     rows = block * heads_dev
     half = key_rows.shape[1]
+    codes = block_codes.T
     pr = block // ni
     total = STEPS + 1
     sems = 2 * (ni - 1) + 2 * (no - 1) + 2 * (2 * ni - 1) + 4 * STEPS
-    vmem, smem = pl.BlockSpec(memory_space=pltpu.VMEM), pl.BlockSpec(memory_space=pltpu.SMEM)
+    smem = pl.BlockSpec(memory_space=pltpu.SMEM)
+    vmem, hbm = pl.BlockSpec(memory_space=pltpu.VMEM), pl.BlockSpec(memory_space=pltpu.HBM)
     tile = (block, dim)
-    grad_q, grad_k, grad_v = pl.pallas_call(
+    grad_q, grad_kv = pl.pallas_call(
         functools.partial(kernel, (ni, no, heads_dev)),
         out_shape=(
-            jax.ShapeDtypeStruct((rows, dim), f32),
-            jax.ShapeDtypeStruct((block, half), f32),
-            jax.ShapeDtypeStruct((block, half), f32),
+            pltpu.VMEM((rows, dim), f32),
+            pltpu.VMEM((2 * half, block), f32),
         ),
-        in_specs=[smem] * 3 + [vmem] * 4,
-        out_specs=(vmem,) * 3,
+        in_specs=[smem] * 2 + [hbm] * 5,
+        out_specs=(vmem,) * 2,
         scratch_shapes=[
+            pltpu.SMEM(codes.shape, jnp.int32),
+            pltpu.VMEM((rows, dim), f32),
+            pltpu.VMEM((rows, dim), f32),
+            pltpu.SemaphoreType.DMA((5,)),
             pltpu.VMEM((STEPS, 2) + tile, f32),
             pltpu.VMEM((2,) + tile, f32),
             pltpu.VMEM((pr, dim), f32),
@@ -373,13 +394,25 @@
             pltpu.SemaphoreType.DMA((sems,)),
         ],
         compiler_params=pltpu.CompilerParams(
-            collective_id=0, has_side_effects=True, vmem_limit_bytes=48 << 20
+            collective_id=0, has_side_effects=True, vmem_limit_bytes=66_000_000
         ),
     )(
-        sink_len, window_len, block_codes,
-        queries.reshape(rows, dim), key_rows, values, out_grad.reshape(rows, dim),
+        sink_len, window_len, codes,
+        queries.reshape(rows, dim), key_rows.T, values.T, out_grad.reshape(rows, dim),
     )
-    return grad_q.reshape(queries.shape), grad_k, grad_v
+    grad_q, grad_k, grad_v = pl.pallas_call(
+        store,
+        out_shape=(
+            jax.ShapeDtypeStruct((rows, dim), f32),
+            jax.ShapeDtypeStruct((half, block), f32),
+            jax.ShapeDtypeStruct((half, block), f32),
+        ),
+        in_specs=[vmem] * 2,
+        out_specs=(hbm,) * 3,
+        scratch_shapes=[pltpu.SemaphoreType.DMA((3,))],
+        compiler_params=pltpu.CompilerParams(vmem_limit_bytes=1 << 20),
+    )(grad_q, grad_kv)
+    return grad_q.reshape(queries.shape), grad_k.T, grad_v.T
 
 
 def solution(mesh):

time: 46 us -> 39.4 us (0.86)
  local copies, waits for them, and re-layouts: 5.03 us -> 0 us
  Pallas kernels: 38.7 us -> 37.3 us
    unnamed x14 -> x0, local copies, waits for them, and re-layouts: 5.03 us -> none
    pallas_call x1, Pallas kernels: 38.7 us -> 36.5 us  [shards(): pl.pallas_call(functools.partial(kernel, (ni, no, heads_dev)), out_shape=...]
    pallas_call x0 -> x1, Pallas kernels: none -> 0.74 us  [shards(): pl.pallas_call(store, out_shape=(jax.ShapeDtypeStruct((rows, dim), f32),...]
where the time goes in v2:
time: 39.4 us; the launch traced here: 39.2 us
  Pallas kernels  37.3 us (95%)
  between operations  1.93 us (5%)
    pallas_call x1, Pallas kernels, shards(): pl.pallas_call(functools.partial(kernel, (ni, no, heads_dev)), out_shape=...  36.5 us

profile of v2, /device:TPU:0, one launch (start us, length us, event | category | flops | bytes accessed | tf_op | source)
XLA Modules:
  0.0 39.2 jit_solution(4237101809775376995)
XLA Ops:
  1.9 36.5 %shard_map.94 = (f32[512,128]{1,0:T(8,128)S(1)}, f32[128,128]{1,0:T(8,128)S(1)}) custom-call(s32[1]{0:T(128)S(6)} %copy.10.sink_ref, s32[1]{0:T(128)S(6)} %copy.11.window_ref, s32[5,16]{1,0:T(8,128)} %bitcast.12, f32[512,128]{1,0:T(8,128)} %bitcast.8, f32[64,128]{1,0:T(8,128)} %bitcast.10, f32[64,128]{1,0:T(8,128)} %bitcast.11, f32[512,128]{1,0:T(8,128)} %bitcast.9), custom_call_target="tpu_custom_call" | custom-call | tf_op jit(solution)/shard_map/pallas_call | solution.py:357
  38.5 0.7 %shard_map.95 = (f32[512,128]{1,0:T(8,128)}, f32[64,128]{1,0:T(8,128)}, f32[64,128]{1,0:T(8,128)}) custom-call(f32[512,128]{1,0:T(8,128)S(1)} %get-tuple-element.8.dq_ref, f32[128,128]{1,0:T(8,128)S(1)} %get-tuple-element.9.dkv_ref), custom_call_target="tpu_custom_call" | custom-call | tf_op jit(solution)/shard_map/pallas_call | solution.py:403

commit v3 on v2

--- a/solution.py
+++ b/solution.py
@@ -36,8 +36,8 @@
 
 def kernel(
     sizes, sink_ref, window_ref, codes_hbm, q_hbm, k_hbm, v_hbm, g_hbm, dq_ref, dkv_ref,
-    codes_ref, q_ref, g_ref, load, buf, sinkb, piece, qcat, gcat, st, dp, dshi, dslo, ktcat,
-    xout, xin, mine, gout, gin, g4out, g4in, sg, sin, s2, s2in, s3, s3in, send, recv,
+    codes_ref, q_ref, g_ref, load, own, buf, sinkb, piece, qcat, gcat, st, dp, dshi, dslo, ktcat,
+    xout, xin, mine, gout, gin, g4out, g4in, fin, sg, sin, s2, s2in, s3, s3in, send, recv,
 ):
     ni, no, heads_dev = sizes
     half, block = k_hbm.shape
@@ -87,9 +87,9 @@
         copy(name, dst, dst, across).wait_recv()
 
     moves = [
-        (k_hbm, buf.at[0, par, 0:half]), (v_hbm, buf.at[0, par, half:2 * half]),
-        (q_hbm, q_ref), (g_hbm, g_ref),
-        (codes_hbm, codes_ref),
+        (k_hbm, buf.at[0, 0, par]), (v_hbm, buf.at[1, 0, par]),
+        (k_hbm, own.at[0:half]), (v_hbm, own.at[half:2 * half]),
+        (q_hbm, q_ref), (g_hbm, g_ref), (codes_hbm, codes_ref),
     ]
     loads = [pltpu.make_async_copy(x, y, load.at[i]) for i, (x, y) in enumerate(moves)]
     for x in loads:
@@ -110,7 +110,6 @@
     gcat[...] = jnp.concatenate([g0, g1, g0, g1, g2, g0], 1)
     pl.semaphore_wait(barrier, len(greet))
 
-    own = buf.at[0, par]
     first = (inner == 0) & (outer == 0)
     top = outer == 0
     at_root = piece
@@ -119,22 +118,27 @@
     def _():
         for i in range(1, ni):
             copy(f"f1_{i}", own.at[pl.ds(i * pr, pr)], at_root, (head, i, outer)).start()
-        piece[...] = buf[0, par, 0:pr, :]
-
-    start("x0", own, own, across)
-    for o in range(FAR, 0, -1):
-        start(f"w{o}", own, buf.at[o, par], seq(o))
-
-    def scores_of(a, c, index, allowed):
-        keys = jnp.concatenate([a[0:half], c[0:half]], 0)
-        vals = jnp.concatenate([a[half:], c[half:]], 0)
+        piece[...] = own[0:pr, :]
+
+    for kind in range(2):
+        mine_kv = buf.at[kind, 0, par]
+        start(f"x0{kind}", mine_kv, mine_kv, across)
+        for o in range(FAR, 0, -1):
+            start(f"w{o}{kind}", mine_kv, buf.at[kind, o, par], seq(o))
+
+    def scores_of(keys, index, allowed):
         k0, k1, k2 = three(keys.T)
-        v0, v1, v2 = three(vals.T)
         s = dot(jnp.concatenate([k0, k0, k1, k1, k0, k2], 1), qcat[...], NT)
         st[index] = jnp.where(allowed, temper * s, very_low)
-        dp[index] = dot(jnp.concatenate([v0, v0, v1, v1, v0, v2], 1), gcat[...], NT)
         t0, t1 = two(keys * temper)
         ktcat[index] = jnp.concatenate([t0, t1, t0], 1)
+
+    def products_of(vals, index):
+        v0, v1, v2 = three(vals.T)
+        dp[index] = dot(jnp.concatenate([v0, v0, v1, v1, v0, v2], 1), gcat[...], NT)
+
+    def joined(kind, o):
+        return jnp.concatenate([buf[kind, o, 0], buf[kind, o, 1]], 0)
 
     jk = lax.broadcasted_iota(jnp.int32, (block, rows), 0)
     iq = lax.broadcasted_iota(jnp.int32, (block, rows), 1) // heads_dev
@@ -151,10 +155,17 @@
         return (gap < limit) & (jk >= here)
 
     def slot(o):
-        scores_of(buf[o, 0], buf[o, 1], o, mask_of(o))
-
-    arrived("x0", buf.at[0, other])
-    start("w4x", buf.at[0, other], buf.at[FAR, other], seq(FAR))
+        scores_of(joined(0, o), o, mask_of(o))
+
+    def far_other(kind):
+        arrived(f"x0{kind}", buf.at[kind, 0, other])
+        start(f"w4x{kind}", buf.at[kind, 0, other], buf.at[kind, FAR, other], seq(FAR))
+
+    def relay(kind, o):
+        arrived(f"w{o}{kind}", buf.at[kind, o, par])
+        start(f"r{o}{kind}", buf.at[kind, o, par], buf.at[kind, o, par], across)
+
+    far_other(0)
 
     @pl.when(top)
     def _():
@@ -169,8 +180,8 @@
 
     slot(0)
     for o in range(1, FAR):
-        arrived(f"w{o}", buf.at[o, par])
-        start(f"r{o}", buf.at[o, par], buf.at[o, par], across)
+        relay(0, o)
+    far_other(1)
 
     @pl.when(outer != 0)
     def _():
@@ -184,76 +195,116 @@
         start(f"f3_{p}_{d}", piece, sinkb.at[par, where], column(p, d))
     sinkb[par, where] = piece[...]
 
-    arrived(f"w{FAR}", buf.at[FAR, par])
-    arrived("w4x", buf.at[FAR, other])
+    arrived(f"w{FAR}0", buf.at[0, FAR, par])
+    arrived("w4x0", buf.at[0, FAR, other])
     slot(FAR)
     for o in range(1, FAR):
-        arrived(f"r{o}", buf.at[o, other])
+        relay(1, o)
+    for o in range(1, FAR):
+        arrived(f"r{o}0", buf.at[0, o, other])
         slot(o)
     for p, d in columns:
         there = pl.ds(pl.multiple_of(source(d) * pr, pr), pr)
         arrived(f"f3_{p}_{d}", sinkb.at[other if p else par, there])
-    scores_of(sinkb[0], sinkb[1], STEPS, jk < jnp.where(b >= 1, sink_end, 0))
+    scores_of(
+        jnp.concatenate([sinkb[0, 0:half], sinkb[1, 0:half]], 0),
+        STEPS, jk < jnp.where(b >= 1, sink_end, 0),
+    )
 
     total = STEPS + 1
     top_score = jnp.max(st[0], axis=0, keepdims=True)
     for i in range(1, total):
         top_score = jnp.maximum(top_score, jnp.max(st[i], axis=0, keepdims=True))
     norm = jnp.zeros((1, rows), f32)
-    delta = jnp.zeros((1, rows), f32)
     for i in range(total):
         e = jnp.exp(st[i] - top_score)
         st[i] = e
         norm = norm + jnp.sum(e, axis=0, keepdims=True)
-        delta = delta + jnp.sum(e * dp[i], axis=0, keepdims=True)
     scale = 1.0 / norm
-    delta = delta * scale
-
-    def grads(i):
+    w = 2 * half
+
+    def parted(grad):
+        low, high = grad[0:half], grad[half:]
+        return jnp.where(par == 0, low, high), jnp.where(par == 0, high, low)
+
+    def value_grad(i):
         probs = st[i] * scale
-        ds = probs * (dp[i] - delta)
-        p_hi, p_lo = two(probs)
-        d_hi, d_lo = two(ds)
-        dshi[i] = d_hi
-        dslo[i] = d_lo
-        w = 2 * half
-        pv = dot(p_hi, gcat[:, 0:2 * w], NN)
-        dv = pv[:, 0:w] + pv[:, w:] + dot(p_lo, gcat[:, 0:w], NN)
-        kq = dot(d_hi, qcat[:, 0:2 * w], NN)
-        dk = temper * (kq[:, 0:w] + kq[:, w:] + dot(d_lo, qcat[:, 0:w], NN))
-        dk, dv = dk.T, dv.T
-        even = jnp.concatenate([dk[0:half], dv[0:half]], 0)
-        odd = jnp.concatenate([dk[half:], dv[half:]], 0)
-        keep = jnp.where(par == 0, even, odd)
-        give = jnp.where(par == 0, odd, even)
-        return keep, give
-
-    keep, give = grads(STEPS)
-    sg[0] = keep
-    sg[1] = give
+        st[i] = probs
+        hi, lo = two(probs)
+        both = dot(hi, gcat[:, 0:2 * w], NN)
+        return parted((both[:, 0:w] + both[:, w:] + dot(lo, gcat[:, 0:w], NN)).T)
+
+    def far_grad(kind, keep, give):
+        g4out[kind, 0] = keep
+        g4out[kind, 1] = give
+        start(f"g4k{kind}", g4out.at[kind, 0], g4in.at[kind, 0], seq(-FAR))
+        start(f"g4g{kind}", g4out.at[kind, 1], g4in.at[kind, 1], seq(-FAR))
+
+    def near_grad(kind, o, keep, give):
+        mine[kind, o] = keep
+        xout[kind, o] = give
+        start(f"gx{o}{kind}", xout.at[kind, o], xin.at[kind, o], across)
+
+    def own_grad(kind, keep, give):
+        arrived(f"g4g{kind}", g4in.at[kind, 1])
+        near_grad(kind, 0, keep, give + g4in[kind, 1])
+
+    def pass_on(kind, o):
+        arrived(f"gx{o}{kind}", xin.at[kind, o])
+        gout[kind, o] = mine[kind, o] + xin[kind, o]
+        start(f"gz{o}{kind}", gout.at[kind, o], gin.at[kind, o], seq(-o))
+
+    near = list(range(FAR - 1, 0, -1))
+    for o in near:
+        near_grad(1, o, *value_grad(o))
+    far_grad(1, *value_grad(FAR))
+    sg[0, half:w], sg[1, half:w] = value_grad(STEPS)
+
+    delta = jnp.zeros((1, rows), f32)
+
+    def weigh(i, delta):
+        return delta + jnp.sum(st[i] * dp[i], axis=0, keepdims=True)
+
+    products_of(jnp.concatenate([sinkb[0, half:], sinkb[1, half:]], 0), STEPS)
+    delta = weigh(STEPS, delta)
+    arrived(f"w{FAR}1", buf.at[1, FAR, par])
+    arrived("w4x1", buf.at[1, FAR, other])
+    products_of(joined(1, FAR), FAR)
+    delta = weigh(FAR, delta)
+    pass_on(1, FAR - 1)
+    own_grad(1, *value_grad(0))
+    products_of(joined(1, 0), 0)
+    delta = weigh(0, delta)
+    for o in range(1, FAR):
+        arrived(f"r{o}1", buf.at[1, o, other])
+        products_of(joined(1, o), o)
+        delta = weigh(o, delta)
+        if o < FAR - 1:
+            pass_on(1, FAR - 1 - o)
+
+    def key_grad(i):
+        hi, lo = two(st[i] * (dp[i] - delta))
+        dshi[i] = hi
+        dslo[i] = lo
+        both = dot(hi, qcat[:, 0:2 * w], NN)
+        grad = temper * (both[:, 0:w] + both[:, w:] + dot(lo, qcat[:, 0:w], NN))
+        return parted(grad.T)
+
+    sg[0, 0:half], sg[1, 0:half] = key_grad(STEPS)
     for p, d in columns:
         target = lax.rem(inner + d, ni)
         rng = pl.ds(pl.multiple_of(target * pr, pr), pr)
         start(f"b1_{p}_{d}", sg.at[p, rng], sin.at[p * ni + d], column(p, d))
 
-    keep, give = grads(FAR)
-    g4out[0] = keep
-    g4out[1] = give
-    start("g4k", g4out.at[0], g4in.at[0], seq(-FAR))
-    start("g4g", g4out.at[1], g4in.at[1], seq(-FAR))
-
-    def pass_on(o):
-        arrived(f"gx{o}", xin.at[o])
-        gout[o] = mine[o] + xin[o]
-        start(f"gz{o}", gout.at[o], gin.at[o], seq(-o))
-
-    for o in range(FAR - 1, 0, -1):
-        keep, give = grads(o)
-        mine[o] = keep
-        xout[o] = give
-        start(f"gx{o}", xout.at[o], xin.at[o], across)
-        if o < FAR - 1:
-            pass_on(o + 1)
+    for o in near:
+        near_grad(0, o, *key_grad(o))
+    far_grad(0, *key_grad(FAR))
+    pass_on(0, near[0])
+    keep, give = key_grad(0)
+    own_grad(0, keep, give)
+    for o in near[1:]:
+        pass_on(0, o)
+
     for p, d in columns:
         arrived(f"b1_{p}_{d}", sin.at[p * ni + d])
     acc = sg[0, where]
@@ -265,14 +316,6 @@
         def _():
             copy(f"b2_{z}", s2, s2in.at[z], (head, inner, 0)).start()
 
-    keep, give = grads(0)
-    arrived("g4g", g4in.at[1])
-    xout[0] = give + g4in[1]
-    start("gx0", xout.at[0], xin.at[0], across)
-    pass_on(1)
-    arrived("g4k", g4in.at[0])
-    mine[0] = keep + g4in[0]
-
     dqt = jnp.zeros((2 * half, rows), f32)
     for i in range(total):
         hi = dshi[i]
@@ -291,21 +334,23 @@
             def _():
                 copy(f"b3_{i}", s3, s3in.at[i], (head, 0, outer)).start()
 
-    arrived("gx0", xin.at[0])
-    acc = mine[0] + xin[0]
-    for o in range(FAR - 1, 0, -1):
-        arrived(f"gz{o}", gin.at[o])
-        acc = acc + gin[o]
-    mine[0] = acc
+    for kind in range(1, -1, -1):
+        arrived(f"g4k{kind}", g4in.at[kind, 0])
+        arrived(f"gx0{kind}", xin.at[kind, 0])
+        acc = mine[kind, 0] + g4in[kind, 0] + xin[kind, 0]
+        for o in near:
+            arrived(f"gz{o}{kind}", gin.at[kind, o])
+            acc = acc + gin[kind, o]
+        fin[kind * half:(kind + 1) * half] = acc
 
     @pl.when(first)
     def _():
-        mine[0, 0:pr] += s3[...]
+        fin[0:pr] += s3[...]
         for i in range(1, ni):
             arrived(f"b3_{i}", s3in.at[i])
-            mine[0, i * pr:(i + 1) * pr] += s3in[i]
-
-    dkv_ref[...] = mine[0]
+            fin[i * pr:(i + 1) * pr] += s3in[i]
+
+    dkv_ref[...] = fin[...]
 
     for c in pending:
         c.wait_send()
@@ -350,7 +395,7 @@
     codes = block_codes.T
     pr = block // ni
     total = STEPS + 1
-    sems = 2 * (ni - 1) + 2 * (no - 1) + 2 * (2 * ni - 1) + 4 * STEPS
+    sems = 2 * (ni - 1) + 2 * (no - 1) + 2 * (2 * ni - 1) + 8 * STEPS
     smem = pl.BlockSpec(memory_space=pltpu.SMEM)
     vmem, hbm = pl.BlockSpec(memory_space=pltpu.VMEM), pl.BlockSpec(memory_space=pltpu.HBM)
     tile = (block, dim)
@@ -366,8 +411,9 @@
             pltpu.SMEM(codes.shape, jnp.int32),
             pltpu.VMEM((rows, dim), f32),
             pltpu.VMEM((rows, dim), f32),
-            pltpu.SemaphoreType.DMA((5,)),
-            pltpu.VMEM((STEPS, 2) + tile, f32),
+            pltpu.SemaphoreType.DMA((7,)),
+            pltpu.VMEM(tile, f32),
+            pltpu.VMEM((2, STEPS, 2, half, block), f32),
             pltpu.VMEM((2,) + tile, f32),
             pltpu.VMEM((pr, dim), f32),
             pltpu.VMEM((rows, 6 * dim), bf16),
@@ -377,13 +423,14 @@
             pltpu.VMEM((total, block, rows), bf16),
             pltpu.VMEM((total, block, rows), bf16),
             pltpu.VMEM((total, dim, 3 * block), bf16),
-            pltpu.VMEM((FAR,) + tile, f32),
-            pltpu.VMEM((FAR,) + tile, f32),
-            pltpu.VMEM((FAR,) + tile, f32),
-            pltpu.VMEM((FAR,) + tile, f32),
-            pltpu.VMEM((FAR,) + tile, f32),
-            pltpu.VMEM((2,) + tile, f32),
-            pltpu.VMEM((2,) + tile, f32),
+            pltpu.VMEM((2, FAR, half, block), f32),
+            pltpu.VMEM((2, FAR, half, block), f32),
+            pltpu.VMEM((2, FAR, half, block), f32),
+            pltpu.VMEM((2, FAR, half, block), f32),
+            pltpu.VMEM((2, FAR, half, block), f32),
+            pltpu.VMEM((2, 2, half, block), f32),
+            pltpu.VMEM((2, 2, half, block), f32),
+            pltpu.VMEM(tile, f32),
             pltpu.VMEM((2,) + tile, f32),
             pltpu.VMEM((2 * ni, pr, dim), f32),
             pltpu.VMEM((pr, dim), f32),

time: 39.4 us -> 42.1 us (1.069)
  Pallas kernels: 37.3 us -> 40 us
    pallas_call x1, Pallas kernels: 36.5 us -> 39.2 us  [shards(): pl.pallas_call(functools.partial(kernel, (ni, no, heads_dev)), out_shape=...]
where the time goes in v3:
time: 42.1 us; the launch traced here: 41.9 us
  Pallas kernels  40 us (95%)
  between operations  1.93 us (5%)
    pallas_call x1, Pallas kernels, shards(): pl.pallas_call(functools.partial(kernel, (ni, no, heads_dev)), out_shape=...  39.2 us

profile of v3, /device:TPU:0, one launch (start us, length us, event | category | flops | bytes accessed | tf_op | source)
XLA Modules:
  0.0 41.9 jit_solution(3404950554904396871)
XLA Ops:
  1.9 39.2 %shard_map.94 = (f32[512,128]{1,0:T(8,128)S(1)}, f32[128,128]{1,0:T(8,128)S(1)}) custom-call(s32[1]{0:T(128)S(6)} %copy.10.sink_ref, s32[1]{0:T(128)S(6)} %copy.11.window_ref, s32[5,16]{1,0:T(8,128)} %bitcast.12, f32[512,128]{1,0:T(8,128)} %bitcast.8, f32[64,128]{1,0:T(8,128)} %bitcast.10, f32[64,128]{1,0:T(8,128)} %bitcast.11, f32[512,128]{1,0:T(8,128)} %bitcast.9), custom_call_target="tpu_custom_call" | custom-call | tf_op jit(solution)/shard_map/pallas_call | solution.py:402
  41.1 0.7 %shard_map.95 = (f32[512,128]{1,0:T(8,128)}, f32[64,128]{1,0:T(8,128)}, f32[64,128]{1,0:T(8,128)}) custom-call(f32[512,128]{1,0:T(8,128)S(1)} %get-tuple-element.8.dq_ref, f32[128,128]{1,0:T(8,128)S(1)} %get-tuple-element.9.dkv_ref), custom_call_target="tpu_custom_call" | custom-call | tf_op jit(solution)/shard_map/pallas_call | solution.py:450

commit v4 on v2

--- a/solution.py
+++ b/solution.py
@@ -35,7 +35,7 @@
 
 
 def kernel(
-    sizes, sink_ref, window_ref, codes_hbm, q_hbm, k_hbm, v_hbm, g_hbm, dq_ref, dkv_ref,
+    sizes, limits_ref, codes_hbm, q_hbm, k_hbm, v_hbm, g_hbm, dq_ref, dkv_ref,
     codes_ref, q_ref, g_ref, load, buf, sinkb, piece, qcat, gcat, st, dp, dshi, dslo, ktcat,
     xout, xin, mine, gout, gin, g4out, g4in, sg, sin, s2, s2in, s3, s3in, send, recv,
 ):
@@ -139,7 +139,7 @@
     jk = lax.broadcasted_iota(jnp.int32, (block, rows), 0)
     iq = lax.broadcasted_iota(jnp.int32, (block, rows), 1) // heads_dev
     gap = iq - jk
-    sink_end, window = sink_ref[0], window_ref[0]
+    sink_end, window = limits_ref[0], limits_ref[1]
 
     def mask_of(o):
         code = codes_ref[o, b]
@@ -168,9 +168,27 @@
             copy(f"f2_{z}", piece, piece, (head, inner, z)).start()
 
     slot(0)
-    for o in range(1, FAR):
-        arrived(f"w{o}", buf.at[o, par])
-        start(f"r{o}", buf.at[o, par], buf.at[o, par], across)
+    def relay(order):
+        for o in order:
+            arrived(f"w{o}", buf.at[o, par])
+            copy(f"r{o}", buf.at[o, par], buf.at[o, par], across).start()
+
+    up = list(range(1, FAR))
+
+    @pl.when(outer == 0)
+    def _():
+        relay(up[::-1])
+
+    @pl.when(outer == no - 1)
+    def _():
+        relay(up)
+
+    @pl.when((outer != 0) & (outer != no - 1))
+    def _():
+        relay(up[::2] + up[1::2])
+
+    for o in up:
+        pending.append(copy(f"r{o}", buf.at[o, par], buf.at[o, par], across))
 
     @pl.when(outer != 0)
     def _():
@@ -228,6 +246,18 @@
         give = jnp.where(par == 0, odd, even)
         return keep, give
 
+    def pass_on(o):
+        arrived(f"gx{o}", xin.at[o])
+        gout[o] = mine[o] + xin[o]
+        start(f"gz{o}", gout.at[o], gin.at[o], seq(-o))
+
+    def near(o):
+        keep, give = grads(o)
+        mine[o] = keep
+        xout[o] = give
+        start(f"gx{o}", xout.at[o], xin.at[o], across)
+
+    near(FAR - 1)
     keep, give = grads(STEPS)
     sg[0] = keep
     sg[1] = give
@@ -236,24 +266,17 @@
         rng = pl.ds(pl.multiple_of(target * pr, pr), pr)
         start(f"b1_{p}_{d}", sg.at[p, rng], sin.at[p * ni + d], column(p, d))
 
+    near(FAR - 2)
+    pass_on(FAR - 1)
     keep, give = grads(FAR)
     g4out[0] = keep
     g4out[1] = give
     start("g4k", g4out.at[0], g4in.at[0], seq(-FAR))
     start("g4g", g4out.at[1], g4in.at[1], seq(-FAR))
 
-    def pass_on(o):
-        arrived(f"gx{o}", xin.at[o])
-        gout[o] = mine[o] + xin[o]
-        start(f"gz{o}", gout.at[o], gin.at[o], seq(-o))
-
-    for o in range(FAR - 1, 0, -1):
-        keep, give = grads(o)
-        mine[o] = keep
-        xout[o] = give
-        start(f"gx{o}", xout.at[o], xin.at[o], across)
-        if o < FAR - 1:
-            pass_on(o + 1)
+    for o in range(FAR - 3, 0, -1):
+        near(o)
+        pass_on(o + 1)
     for p, d in columns:
         arrived(f"b1_{p}_{d}", sin.at[p * ni + d])
     acc = sg[0, where]
@@ -360,7 +383,7 @@
             pltpu.VMEM((rows, dim), f32),
             pltpu.VMEM((2 * half, block), f32),
         ),
-        in_specs=[smem] * 2 + [hbm] * 5,
+        in_specs=[smem] + [hbm] * 5,
         out_specs=(vmem,) * 2,
         scratch_shapes=[
             pltpu.SMEM(codes.shape, jnp.int32),
@@ -397,7 +420,7 @@
             collective_id=0, has_side_effects=True, vmem_limit_bytes=66_000_000
         ),
     )(
-        sink_len, window_len, codes,
+        jnp.concatenate([sink_len, window_len]), codes,
         queries.reshape(rows, dim), key_rows.T, values.T, out_grad.reshape(rows, dim),
     )
     grad_q, grad_k, grad_v = pl.pallas_call(

time: 39.4 us -> 40 us (1.015)
  other arithmetic: 0 us -> 0.59 us
    concatenate x0 -> x1, other arithmetic: none -> 0.59 us  [shards(): jnp.concatenate([sink_len, window_len])]
where the time goes in v4:
time: 40 us; the launch traced here: 39.8 us
  Pallas kernels  37.3 us (93%)
  between operations  1.93 us (5%)
  other arithmetic  0.59 us (1%)
    pallas_call x1, Pallas kernels, shards(): pl.pallas_call(functools.partial(kernel, (ni, no, heads_dev)), out_shape=...  36.6 us

profile of v4, /device:TPU:0, one launch (start us, length us, event | category | flops | bytes accessed | tf_op | source)
XLA Modules:
  0.0 39.8 jit_solution(6102416617866441870)
XLA Ops:
  1.9 0.6 %pad_add_fusion.limits_ref = s32[2]{0:T(128)} fusion(s32[1]{0:T(128)S(6)} %copy.11, s32[1]{0:T(128)S(6)} %copy.10), kind=kLoop, calls=%fused_computation | loop fusion | flops 2 | bytes 16 | tf_op jit(solution)/shard_map/concatenate | solution.py:423
  2.5 36.6 %shard_map.94 = (f32[512,128]{1,0:T(8,128)S(1)}, f32[128,128]{1,0:T(8,128)S(1)}) custom-call(s32[2]{0:T(128)} %pad_add_fusion.limits_ref, s32[5,16]{1,0:T(8,128)} %bitcast.12, f32[512,128]{1,0:T(8,128)} %bitcast.8, f32[64,128]{1,0:T(8,128)} %bitcast.10, f32[64,128]{1,0:T(8,128)} %bitcast.11, f32[512,128]{1,0:T(8,128)} %bitcast.9), custom_call_target="tpu_custom_call" | custom-call | tf_op jit(solution)/shard_map/pallas_call | solution.py:380
  39.1 0.7 %shard_map.95 = (f32[512,128]{1,0:T(8,128)}, f32[64,128]{1,0:T(8,128)}, f32[64,128]{1,0:T(8,128)}) custom-call(f32[512,128]{1,0:T(8,128)S(1)} %get-tuple-element.8.dq_ref, f32[128,128]{1,0:T(8,128)S(1)} %get-tuple-element.9.dkv_ref), custom_call_target="tpu_custom_call" | custom-call | tf_op jit(solution)/shard_map/pallas_call | solution.py:426

commit v5 on v4

--- a/solution.py
+++ b/solution.py
@@ -35,7 +35,7 @@
 
 
 def kernel(
-    sizes, limits_ref, codes_hbm, q_hbm, k_hbm, v_hbm, g_hbm, dq_ref, dkv_ref,
+    sizes, sink_ref, window_ref, codes_hbm, q_hbm, k_hbm, v_hbm, g_hbm, dq_ref, dkv_ref,
     codes_ref, q_ref, g_ref, load, buf, sinkb, piece, qcat, gcat, st, dp, dshi, dslo, ktcat,
     xout, xin, mine, gout, gin, g4out, g4in, sg, sin, s2, s2in, s3, s3in, send, recv,
 ):
@@ -139,7 +139,7 @@
     jk = lax.broadcasted_iota(jnp.int32, (block, rows), 0)
     iq = lax.broadcasted_iota(jnp.int32, (block, rows), 1) // heads_dev
     gap = iq - jk
-    sink_end, window = limits_ref[0], limits_ref[1]
+    sink_end, window = sink_ref[0], window_ref[0]
 
     def mask_of(o):
         code = codes_ref[o, b]
@@ -257,7 +257,6 @@
         xout[o] = give
         start(f"gx{o}", xout.at[o], xin.at[o], across)
 
-    near(FAR - 1)
     keep, give = grads(STEPS)
     sg[0] = keep
     sg[1] = give
@@ -266,6 +265,7 @@
         rng = pl.ds(pl.multiple_of(target * pr, pr), pr)
         start(f"b1_{p}_{d}", sg.at[p, rng], sin.at[p * ni + d], column(p, d))
 
+    near(FAR - 1)
     near(FAR - 2)
     pass_on(FAR - 1)
     keep, give = grads(FAR)
@@ -383,7 +383,7 @@
             pltpu.VMEM((rows, dim), f32),
             pltpu.VMEM((2 * half, block), f32),
         ),
-        in_specs=[smem] + [hbm] * 5,
+        in_specs=[smem] * 2 + [hbm] * 5,
         out_specs=(vmem,) * 2,
         scratch_shapes=[
             pltpu.SMEM(codes.shape, jnp.int32),
@@ -420,7 +420,7 @@
             collective_id=0, has_side_effects=True, vmem_limit_bytes=66_000_000
         ),
     )(
-        jnp.concatenate([sink_len, window_len]), codes,
+        sink_len, window_len, codes,
         queries.reshape(rows, dim), key_rows.T, values.T, out_grad.reshape(rows, dim),
     )
     grad_q, grad_k, grad_v = pl.pallas_call(

time: 40 us -> 38.6 us (0.965)
  Pallas kernels: 37.3 us -> 36.5 us
  other arithmetic: 0.59 us -> 0 us
    pallas_call x1, Pallas kernels: 36.6 us -> 35.8 us  [shards(): pl.pallas_call(functools.partial(kernel, (ni, no, heads_dev)), out_shape=...]
    concatenate x1 -> x0, other arithmetic: 0.59 us -> none  [shards(): jnp.concatenate([sink_len, window_len])]
where the time goes in v5:
time: 38.6 us; the launch traced here: 38.4 us
  Pallas kernels  36.5 us (95%)
  between operations  1.93 us (5%)
    pallas_call x1, Pallas kernels, shards(): pl.pallas_call(functools.partial(kernel, (ni, no, heads_dev)), out_shape=...  35.8 us

profile of v5, /device:TPU:0, one launch (start us, length us, event | category | flops | bytes accessed | tf_op | source)
XLA Modules:
  0.0 38.4 jit_solution(14687665857220855693)
XLA Ops:
  1.9 35.8 %shard_map.94 = (f32[512,128]{1,0:T(8,128)S(1)}, f32[128,128]{1,0:T(8,128)S(1)}) custom-call(s32[1]{0:T(128)S(6)} %copy.10.sink_ref, s32[1]{0:T(128)S(6)} %copy.11.window_ref, s32[5,16]{1,0:T(8,128)} %bitcast.12, f32[512,128]{1,0:T(8,128)} %bitcast.8, f32[64,128]{1,0:T(8,128)} %bitcast.10, f32[64,128]{1,0:T(8,128)} %bitcast.11, f32[512,128]{1,0:T(8,128)} %bitcast.9), custom_call_target="tpu_custom_call" | custom-call | tf_op jit(solution)/shard_map/pallas_call | solution.py:380
  37.7 0.7 %shard_map.95 = (f32[512,128]{1,0:T(8,128)}, f32[64,128]{1,0:T(8,128)}, f32[64,128]{1,0:T(8,128)}) custom-call(f32[512,128]{1,0:T(8,128)S(1)} %get-tuple-element.8.dq_ref, f32[128,128]{1,0:T(8,128)S(1)} %get-tuple-element.9.dkv_ref), custom_call_target="tpu_custom_call" | custom-call | tf_op jit(solution)/shard_map/pallas_call | solution.py:426
